TPU v7x, 32 devices: a whole 2x2x4 slice. The times are simulated.
32 devices in a mesh: groups: 2 (over x), mp: 16 (over z, y, core).
Axes of the slice: x: 2, y: 2, z: 4, core: 2. Of those that a mesh axis runs over, the one named last changes fastest.
Arguments:
- hidden: bfloat16 [1024, 4096], P(('groups', 'mp')), parts along dimension 0, may hold values from -6 to 6
- norm_gain_attn: float32 [4096], replicated, may hold values from 0.5 to 1.5
- w_query: bfloat16 [4096, 1024], P(None, 'mp'), may hold values from -0.09375 to 0.09375
- entering_kv: bfloat16 [16, 2048, 2048], P('groups', 'mp'), parts along dimension 0, may hold values from -60 to 60
- cached_kv: bfloat16 [16, 2048, 2048], P('groups', None, 'mp'), parts along dimension 0, may hold values from -60 to 60
- enc_lengths: int32 [2, 16], P(None, 'groups'), parts along dimension 1, may hold values from 128 to 2048
- w_out: bfloat16 [1024, 4096], P('mp'), may hold values from -0.1875 to 0.1875
- norm_gain_ffn: float32 [4096], replicated, may hold values from 0.5 to 1.5
- w_gate: bfloat16 [4096, 10240], P(None, 'mp'), may hold values from -0.09375 to 0.09375
- w_up: bfloat16 [4096, 10240], P(None, 'mp'), may hold values from -0.09375 to 0.09375
- w_down: bfloat16 [10240, 4096], P('mp'), may hold values from -0.0625 to 0.0625
Outputs:
- output: bfloat16 [1024, 4096], P(('groups', 'mp')), parts along dimension 0
There are 2 independent parts, one for each index of `groups`. A program takes and returns all parts, laid end to end along the dimension named above; an argument that names none is the same for every part. Nothing has to cross between parts.
All inputs are finite; a program needn't handle non-finite values.
Results may differ from a plain program's by a relative error of at most 0.0095.
The roundings to bfloat16 on the way count: a program that leaves them out, or rounds other values in their place, can miss the bound.
Values may be sent and summed in bfloat16 or wider, within the bound.
A program may use at most 128 MiB of HBM per device.

v0:
```python
import jax
import jax.numpy as jnp
from jax import lax
from jax.sharding import PartitionSpec as P

DH = 64
S = 2048
QLEN = 32


epsilon = 0.1


def normalize(matrix, gain_row):
    values = matrix.astype(jnp.float32)
    mean_square = jnp.mean(values * values, axis=-1, keepdims=True)
    return (values * lax.rsqrt(mean_square + epsilon) * gain_row).astype(jnp.bfloat16)


def attend(query, key_value, lengths):
    requests = lengths.shape[0]
    head_count = key_value.shape[2] // (2 * DH)
    query_heads = query.reshape(requests, QLEN, head_count, DH)
    paired = key_value.reshape(requests, S, head_count, 2, DH)
    key_part = paired[:, :, :, 0, :]
    value_part = paired[:, :, :, 1, :]
    scores = jnp.einsum(
        "rqhd,rshd->rhqs", query_heads, key_part, preferred_element_type=jnp.float32
    )
    usable = (jnp.arange(S, dtype=jnp.int32)[None, :] < lengths[:, None])[:, None, None, :]
    masked = jnp.where(usable, scores, -1e30)
    largest = jnp.max(masked, axis=-1, keepdims=True)
    exponent = jnp.where(usable, jnp.exp(masked - largest), 0.0)
    weights = (exponent / jnp.sum(exponent, axis=-1, keepdims=True)).astype(jnp.bfloat16)
    context = jnp.einsum("rhqs,rshd->rqhd", weights, value_part, preferred_element_type=jnp.float32)
    return context.astype(jnp.bfloat16).reshape(requests * QLEN, head_count * DH)


def per_device(
    hidden,
    norm_gain_attn,
    w_query,
    entering_kv,
    cached_kv,
    enc_lengths,
    w_out,
    norm_gain_ffn,
    w_gate,
    w_up,
    w_down,
):
    arrived = lax.all_to_all(entering_kv, "mp", split_axis=2, concat_axis=1, tiled=True)
    query = jnp.dot(
        lax.all_gather(normalize(hidden, norm_gain_attn), "mp", axis=0, tiled=True),
        w_query,
        preferred_element_type=jnp.float32,
    ).astype(jnp.bfloat16)
    split_row = query.shape[0] // 2
    context = jnp.concatenate(
        [
            attend(query[:split_row], arrived, enc_lengths[0]),
            attend(query[split_row:], cached_kv, enc_lengths[1]),
        ],
        axis=0,
    )
    attention = lax.psum_scatter(
        jnp.dot(context, w_out, preferred_element_type=jnp.float32),
        "mp",
        scatter_dimension=0,
        tiled=True,
    )
    residual = (hidden.astype(jnp.float32) + attention).astype(jnp.bfloat16)
    portion = lax.all_gather(normalize(residual, norm_gain_ffn), "mp", axis=0, tiled=True)
    gate = jnp.dot(portion, w_gate, preferred_element_type=jnp.float32)
    upward = jnp.dot(portion, w_up, preferred_element_type=jnp.float32)
    activated = (jax.nn.gelu(gate, approximate=True) * upward).astype(jnp.bfloat16)
    feed_out = lax.psum_scatter(
        jnp.dot(activated, w_down, preferred_element_type=jnp.float32),
        "mp",
        scatter_dimension=0,
        tiled=True,
    )
    return (residual.astype(jnp.float32) + feed_out).astype(jnp.bfloat16)


def solution(mesh):
    placed = (
        P(("groups", "mp"), None),
        P(),
        P(None, "mp"),
        P("groups", "mp", None),
        P("groups", None, "mp"),
        P(None, "groups"),
        P("mp", None),
        P(),
        P(None, "mp"),
        P(None, "mp"),
        P("mp", None),
    )
    return jax.shard_map(
        per_device, mesh=mesh, in_specs=placed, out_specs=P(("groups", "mp"), None), check_vma=False
    )
```

profile of v0, /device:TPU:0, one launch (start us, length us, event | category | flops | bytes accessed | tf_op | source)
XLA Modules:
  0.0 457.6 jit_solution(15572420017858744142)
XLA Ops:
  6.5 0.0 copy-start
  6.5 0.0 all-gather.3.cloned.1.call-start
  6.5 1.2 fusion.23
  7.7 1.8 fusion.25
  9.5 0.0 all-gather.3.cloned.1.call-update
  9.5 6.7 %copy.23 = bf16[8,128,2048]{1,0,2:T(8,128)(2,1)} copy(bf16[8,128,2048]{2,1,0:T(8,128)(2,1)} %param.14) | data formatting | bytes 8388608 | tf_op args[3]
  16.2 7.5 %all-to-all-start = ((bf16[8,128,2048]{1,0,2:T(8,128)(2,1)}), bf16[8,128,2048]{1,0,2:T(8,128)(2,1)}, u32[]{:S(2)}, u32[]{:S(2)}) async-start(bf16[8,128,2048]{1,0,2:T(8,128)(2,1)} %copy.23), calls=%async_computation | async-start | bytes 8388608 | tf_op jit(solution)/shard_map/all_to_all | solution.py:52
  23.7 0.0 copy-start.5
  23.7 0.0 copy-start.3
  23.7 0.0 reduce-scatter.3.cloned.1.call-start
  23.8 6.6 %copy.28 = bf16[8,2048,128]{1,2,0:T(8,128)(2,1)} copy(bf16[8,2048,128]{2,1,0:T(8,128)(2,1)} %param.15) | data formatting | bytes 8388608 | tf_op args[4]
  30.4 0.0 copy-done.5
  30.4 0.1 iota_compare_fusion
  30.5 83.9 %all-gather.3.cloned.1.call-done = bf16[512,4096]{1,0:T(8,128)(2,1)} async-done(((bf16[32,4096]{1,0:T(8,128)(2,1)}), bf16[512,4096]{1,0:T(8,128)(2,1)}) %all-gather.3.cloned.1.call-update) | async-done | bytes 4194320 | tf_op jit(solution)/shard_map/all_gather | solution.py:54
  114.4 0.0 copy-done.3
  114.4 3.6 convolution_convert_fusion
  118.0 0.1 copy.22
  118.1 0.1 copy.27
  118.2 5.8 %all-to-all-done = bf16[8,128,2048]{1,0,2:T(8,128)(2,1)} async-done(((bf16[8,128,2048]{1,0,2:T(8,128)(2,1)}), bf16[8,128,2048]{1,0,2:T(8,128)(2,1)}, u32[]{:S(2)}, u32[]{:S(2)}) %all-to-all-start) | async-done | bytes 4194336 | tf_op jit(solution)/shard_map/all_to_all | solution.py:52
  124.0 6.8 %copy.36 = bf16[8,128,16,128]{1,2,3,0:T(8,128)(2,1)} copy(bf16[8,128,16,128]{1,0,3,2:T(8,128)(2,1)} %bitcast.2) | data formatting | bytes 8388608 | tf_op jit(solution)/shard_map/all_to_all | solution.py:52
  130.8 7.3 %reshape.144 = bf16[8,2048,1,2,64]{1,4,3,0,2:T(8,128)(2,1)} reshape(bf16[8,16,128,128]{2,1,3,0:T(8,128)(2,1)} %bitcast.67) | data formatting | bytes 8388608 | tf_op jit(solution)/shard_map/reshape | solution.py:24
  138.1 2.5 fusion.43
  140.7 2.4 fusion.18
  143.0 2.6 fusion.42
  145.6 2.4 fusion.19
  148.0 0.0 copy-done
  148.0 4.5 fusion.31
  152.5 0.0 copy-start.2
  152.5 0.0 copy-start.4
  152.5 0.0 reduce-scatter.3.cloned.1.call-update
  152.5 0.0 all-gather.5.cloned.1.call-start
  152.5 118.2 %reduce-scatter.3.cloned.1.call-done = f32[32,4096]{1,0:T(8,128)} async-done(((f32[512,4096]{1,0:T(8,128)}), f32[32,4096]{1,0:T(8,128)}) %reduce-scatter.3.cloned.1.call-update) | async-done | bytes 524304 | tf_op jit(solution)/shard_map/reduce_scatter | solution.py:66
  270.8 0.0 copy-done.2
  270.8 1.2 fusion.27
  272.0 0.0 copy-done.4
  272.0 0.8 fusion.29
  272.8 0.0 all-gather.5.cloned.1.call-update
  272.9 0.2 reduce-scatter.5.cloned.1.call-start
  273.1 49.9 %all-gather.5.cloned.1.call-done = bf16[512,4096]{1,0:T(8,128)(2,1)} async-done(((bf16[32,4096]{1,0:T(8,128)(2,1)}), bf16[512,4096]{1,0:T(8,128)(2,1)}) %all-gather.5.cloned.1.call-update) | async-done | bytes 4194320 | tf_op jit(solution)/shard_map/all_gather | solution.py:73
  323.0 6.7 %fusion.44 = f32[512,640]{1,0:T(8,128)S(1)} fusion(bf16[512,4096]{1,0:T(8,128)(2,1)} %all-gather.5.cloned.1.call-done, bf16[4096,640]{1,0:T(8,128)(2,1)} %param.19), kind=kOutput, calls=%fused_computation.67 | convolution fusion | flops 2684354560 | bytes 10747904 | tf_op jit(solution)/shard_map/dot_general | solution.py:74
  329.8 17.3 %fusion.22 = f32[512,4096]{1,0:T(8,128)} fusion(bf16[640,4096]{1,0:T(8,128)(2,1)} %param.21, bf16[512,4096]{1,0:T(8,128)(2,1)} %all-gather.5.cloned.1.call-done, bf16[4096,640]{1,0:T(8,128)(2,1)} %param.20, f32[512,640]{1,0:T(8,128)S(1)} %fusion.44), kind=kOutput, calls=%fused_computation.40 | convolution fusion | flops 5371985920 | bytes 24379392 | tf_op jit(solution)/shard_map/dot_general | solution.py:78
  347.1 0.0 reduce-scatter.5.cloned.1.call-update
  347.1 0.0 copy-start.1
  347.1 102.1 %reduce-scatter.5.cloned.1.call-done = f32[32,4096]{1,0:T(8,128)} async-done(((f32[512,4096]{1,0:T(8,128)}), f32[32,4096]{1,0:T(8,128)}) %reduce-scatter.5.cloned.1.call-update) | async-done | bytes 524304 | tf_op jit(solution)/shard_map/reduce_scatter | solution.py:77
  449.3 1.8 fusion.30
  451.0 0.0 copy-done.1
  (4 shorter events, 0.0 us)
Async XLA Ops:
  6.5 141.5 %copy-start = (bf16[64,4096]{1,0:T(8,128)(2,1)S(1)}, bf16[64,4096]{1,0:T(8,128)(2,1)}, u32[]{:S(2)}) copy-start(bf16[64,4096]{1,0:T(8,128)(2,1)} %param.17) | copy-start | bytes 1572868
  6.5 107.8 %all-gather.3.cloned.1.call-start = ((), (), s32[]{:S(2)}) async-start(), calls=%async_computation.3 | async-start | bytes 4456448 | tf_op jit(solution)/shard_map/all_gather | solution.py:54
  16.2 107.7 %all-to-all-start = ((bf16[8,128,2048]{1,0,2:T(8,128)(2,1)}), bf16[8,128,2048]{1,0,2:T(8,128)(2,1)}, u32[]{:S(2)}, u32[]{:S(2)}) async-start(bf16[8,128,2048]{1,0,2:T(8,128)(2,1)} %copy.23), calls=%async_computation | async-start | bytes 8388608 | tf_op jit(solution)/shard_map/all_to_all | solution.py:52
  23.7 6.7 %copy-start.5 = (s32[2,8]{1,0:T(2,128)S(1)}, s32[2,8]{1,0:T(2,128)}, u32[]{:S(2)}) copy-start(s32[2,8]{1,0:T(2,128)} %param.16) | copy-start | bytes 196
  23.7 90.7 %copy-start.3 = (bf16[4096,64]{0,1:T(8,128)(2,1)S(1)}, bf16[4096,64]{0,1:T(8,128)(2,1)}, u32[]{:S(2)}) copy-start(bf16[4096,64]{0,1:T(8,128)(2,1)} %param.13) | copy-start | bytes 1572868
  23.7 247.0 %reduce-scatter.3.cloned.1.call-start = ((), (), s32[]{:S(2)}) async-start(), calls=%async_computation.4 | async-start | bytes 8912896 | tf_op jit(solution)/shard_map/reduce_scatter | solution.py:66
  152.5 118.3 %copy-start.2 = (bf16[32,4096]{1,0:T(8,128)(2,1)S(1)}, bf16[32,4096]{1,0:T(8,128)(2,1)}, u32[]{:S(2)}) copy-start(bf16[32,4096]{1,0:T(8,128)(2,1)} %param.11) | copy-start | bytes 786436
  152.5 119.5 %copy-start.4 = (f32[4096]{0:T(1024)S(1)}, f32[4096]{0:T(1024)}, u32[]{:S(2)}) copy-start(f32[4096]{0:T(1024)} %param.18) | copy-start | bytes 49156
  152.5 170.6 %all-gather.5.cloned.1.call-start = ((), (), s32[]{:S(2)}) async-start(), calls=%async_computation.5 | async-start | bytes 4456448 | tf_op jit(solution)/shard_map/all_gather | solution.py:73
  272.9 176.4 %reduce-scatter.5.cloned.1.call-start = ((), (), s32[]{:S(2)}) async-start(), calls=%async_computation.6 | async-start | bytes 8912896 | tf_op jit(solution)/shard_map/reduce_scatter | solution.py:77
  347.1 103.9 %copy-start.1 = (bf16[64,4096]{1,0:T(8,128)(2,1)S(1)}, bf16[64,4096]{1,0:T(8,128)(2,1)}, u32[]{:S(2)}) copy-start(bf16[64,4096]{1,0:T(8,128)(2,1)} %param.17) | copy-start | bytes 1572868
Sparse Core Ops, SparseCore 0:
  9.7 104.6 all-gather.2
  152.6 118.1 reduce-scatter.2
  273.0 50.0 all-gather.4
  347.2 101.9 reduce-scatter.4
where the time goes:
time: 458 us
  waiting for transfers between devices  360 us (79%)
  matrix products  41.9 us (9%)
  local copies, waits for them, and re-layouts  27.8 us (6%)
  between operations  13.2 us (3%)
  starting transfers between devices  7.77 us (2%)
  other arithmetic  6.92 us (2%)
    reduce_scatter x1, waiting for transfers between devices, per_device(): lax.psum_scatter(jnp.dot(context, w_out, preferred_element_type=jnp.float...  118 us
    reduce_scatter x1, waiting for transfers between devices, per_device(): lax.psum_scatter(jnp.dot(activated, w_down, preferred_element_type=jnp.fl...  102 us
    all_gather x1, waiting for transfers between devices, per_device(): lax.all_gather(normalize(hidden, norm_gain_attn), 'mp', axis=0, tiled=True)  83.9 us
    all_gather x1, waiting for transfers between devices, per_device(): lax.all_gather(normalize(residual, norm_gain_ffn), 'mp', axis=0, tiled=True)  49.9 us
    dot_general x1, matrix products, per_device(): jnp.dot(activated, w_down, preferred_element_type=jnp.float32)  17.3 us
    unnamed x14, local copies, waits for them, and re-layouts  13.3 us
  transfers between devices with their start and end apart: 5, of which 5 were waited for; matrix products, arithmetic and copies ran while one was open for 4% of the time, Pallas kernels for 0%

commit v1 on v0

v1 whole, which is shorter than its diff:
```python
import functools

import jax
import jax.numpy as jnp
from jax import lax
from jax.experimental import pallas as pl
from jax.experimental.pallas import tpu as pltpu
from jax.sharding import PartitionSpec as P

DH = 64
QLEN = 32
PAD = 2 * DH
MESH = pl.DeviceIdType.MESH
VM = pltpu.VMEM
DMA = pltpu.SemaphoreType.DMA

epsilon = 0.1


def normalize(matrix, gain_row):
    values = matrix.astype(jnp.float32)
    mean_square = jnp.mean(values * values, axis=-1, keepdims=True)
    return (values * lax.rsqrt(mean_square + epsilon) * gain_row).astype(jnp.bfloat16)


def place(n):
    me = lax.axis_index("mp")
    return me, me // 4, (me // 2) % 2, me % 2


def index_of(a, b, c):
    return (a * 2 + b) * 2 + c


def remote(src, dst, send, recv, to):
    return pltpu.make_async_remote_copy(
        src_ref=src, dst_ref=dst, send_sem=send, recv_sem=recv, device_id={"mp": to}, device_id_type=MESH
    )


def greet(to):
    pl.semaphore_signal(pltpu.get_barrier_semaphore(), inc=1, device_id={"mp": to}, device_id_type=MESH)


def gather_kernel(n, x_ref, out_ref, zs, zr, ys, yr, cs, cr):
    A = n // 4
    me, a, b, c = place(n)
    across, pair = index_of(a, 1 - b, c), index_of(a, b, 1 - c)
    right, left = me + 4, me - 4
    has = {1: a < A - 1, -1: a > 0}
    toward = {1: right, -1: left}
    for d in (1, -1):

        @pl.when(has[d])
        def _():
            greet(toward[d])

    greet(across)
    greet(pair)
    pl.semaphore_wait(
        pltpu.get_barrier_semaphore(), 2 + has[1].astype(jnp.int32) + has[-1].astype(jnp.int32)
    )

    def z_copy(src, k, s, d):
        row = 0 if d == 1 else A
        return remote(src, out_ref.at[index_of(k, b, c)], zs.at[row + s], zr.at[k], toward[d])

    def y_copy(src, k, bb):
        return remote(src, out_ref.at[index_of(k, bb, c)], ys.at[k], yr.at[k], across)

    def c_copy(src, k, bb, cc):
        return remote(src, out_ref.at[index_of(k, bb, cc)], cs.at[bb * A + k], cr.at[bb * A + k], pair)

    for d in (1, -1):

        @pl.when(has[d])
        def _():
            z_copy(x_ref, a, 0, d).start()

    y_copy(x_ref, a, b).start()
    c_copy(x_ref, a, b, c).start()
    out_ref[me] = x_ref[...]

    def pass_on(s):
        for d in (1, -1) if s else (1,):
            k = a - s * d

            @pl.when((k >= 0) & (k < A))
            def _():
                y_copy(x_ref, k, 1 - b).wait_recv()
                c_copy(out_ref.at[index_of(k, 1 - b, c)], k, 1 - b, c).start()

    for s in range(1, A):
        for d in (1, -1):
            k = a - s * d

            @pl.when((k >= 0) & (k < A))
            def _():
                block = out_ref.at[index_of(k, b, c)]
                remote(x_ref, block, zs.at[0], zr.at[k], toward[-d]).wait_recv()

                @pl.when(has[d])
                def _():
                    z_copy(block, k, s, d).start()

                y_copy(block, k, b).start()
                c_copy(block, k, b, c).start()

        pass_on(s - 1)
    pass_on(A - 1)
    for bb in range(2):
        for k in range(A):
            c_copy(x_ref, k, bb, 1 - c).wait_recv()
    for s in range(A):
        for d in (1, -1):
            k = a - s * d

            @pl.when((k >= 0) & (k < A) & has[d])
            def _():
                z_copy(x_ref, k, s, d).wait_send()

    for k in range(A):
        y_copy(x_ref, k, b).wait_send()
        for bb in range(2):
            c_copy(x_ref, k, bb, c).wait_send()


def params(number):
    return pltpu.CompilerParams(collective_id=number, has_side_effects=True, vmem_limit_bytes=56 * 2**20)


def gather(x, n, number):
    A = n // 4
    return pl.pallas_call(
        functools.partial(gather_kernel, n),
        out_shape=jax.ShapeDtypeStruct((n,) + x.shape, x.dtype),
        in_specs=[pl.BlockSpec(memory_space=VM)],
        out_specs=pl.BlockSpec(memory_space=VM),
        scratch_shapes=[DMA((2 * A,)), DMA((A,)), DMA((A,)), DMA((A,)), DMA((2 * A,)), DMA((2 * A,))],
        compiler_params=params(number),
        name=f"gather_{number}",
    )(x)


def scatter_kernel(n, part_ref, out_ref, cbuf, ysend, yrecv, zsend, zrecv, cs, cr, ys, yr, zs, zr):
    A = n // 4
    me, a, b, c = place(n)
    across, pair = index_of(a, 1 - b, c), index_of(a, b, 1 - c)
    order = sorted(range(A), key=lambda s: -min(s, A - s))
    for s in range(1, A):
        greet(index_of(lax.rem(a + s, A), b, c))
    greet(across)
    greet(pair)
    pl.semaphore_wait(pltpu.get_barrier_semaphore(), A + 1)

    def c_copy(k, bb, cc):
        slot = bb * A + k
        return remote(part_ref.at[index_of(k, bb, cc)], cbuf.at[slot], cs.at[slot], cr.at[slot], pair)

    def y_copy(k):
        return remote(ysend.at[k], yrecv.at[k], ys.at[k], yr.at[k], across)

    def z_copy(k):
        return remote(zsend.at[k], zrecv.at[a], zs.at[k], zr.at[a], index_of(k, b, c))

    ks = [lax.rem(a + s, A) for s in order]
    for bb in (1 - b, b):
        for k in ks:
            c_copy(k, bb, 1 - c).start()
    for k in ks:
        c_copy(k, 1 - b, 1 - c).wait_recv()
        total = part_ref[index_of(k, 1 - b, c)] + cbuf[(1 - b) * A + k]
        ysend[k] = total.astype(jnp.bfloat16)
        y_copy(k).start()
    for s, k in zip(order, ks):
        c_copy(k, b, 1 - c).wait_recv()
        y_copy(k).wait_recv()
        total = part_ref[index_of(k, b, c)] + cbuf[b * A + k] + yrecv[k].astype(jnp.float32)
        if s:
            zsend[k] = total.astype(jnp.bfloat16)
            z_copy(k).start()
        else:
            out_ref[...] = total
    for s, k in zip(order, ks):
        if s:
            remote(zsend.at[k], zrecv.at[k], zs.at[k], zr.at[k], index_of(k, b, c)).wait_recv()
            out_ref[...] += zrecv[k].astype(jnp.float32)
    for s, k in zip(order, ks):
        y_copy(k).wait_send()
        if s:
            z_copy(k).wait_send()
        for bb in range(2):
            c_copy(k, bb, 1 - c).wait_send()


def scatter(part, n, number):
    A = n // 4
    block = (part.shape[0] // n, part.shape[1])
    half = jnp.bfloat16
    return pl.pallas_call(
        functools.partial(scatter_kernel, n),
        out_shape=jax.ShapeDtypeStruct(block, jnp.float32),
        in_specs=[pl.BlockSpec(memory_space=VM)],
        out_specs=pl.BlockSpec(memory_space=VM),
        scratch_shapes=[VM((2 * A,) + block, jnp.float32)]
        + [VM((A,) + block, half)] * 4
        + [DMA((2 * A,)), DMA((2 * A,)), DMA((A,)), DMA((A,)), DMA((A,)), DMA((A,))],
        compiler_params=params(number),
        name=f"scatter_{number}",
    )(part.reshape((n,) + block))


def exchange_kernel(n, o_ref, st_ref, o_out, st_out, s0, r0, s1, r1):
    me = lax.axis_index("mp")
    for s in range(1, n):
        greet(lax.rem(me + s, n))
    pl.semaphore_wait(pltpu.get_barrier_semaphore(), n - 1)

    def copies(s, mine):
        other = lax.rem(me + s, n)
        spot = me if mine else other
        return (
            remote(o_ref.at[other], o_out.at[spot], s0.at[other], r0.at[spot], other),
            remote(st_ref.at[other], st_out.at[spot], s1.at[other], r1.at[spot], other),
        )

    order = sorted(range(1, n), key=lambda s: -min(s, n - s))
    for s in order:
        for copy in copies(s, True):
            copy.start()
    o_out[me] = o_ref[me]
    st_out[me] = st_ref[me]
    for s in order:
        for copy in copies(s, False):
            copy.wait_recv()
    for s in order:
        for copy in copies(s, True):
            copy.wait_send()


def exchange(o, st, n, number):
    return pl.pallas_call(
        functools.partial(exchange_kernel, n),
        out_shape=(jax.ShapeDtypeStruct(o.shape, o.dtype), jax.ShapeDtypeStruct(st.shape, st.dtype)),
        in_specs=[pl.BlockSpec(memory_space=VM)] * 2,
        out_specs=[pl.BlockSpec(memory_space=VM)] * 2,
        scratch_shapes=[DMA((n,))] * 4,
        compiler_params=params(number),
        name=f"exchange_{number}",
    )(o, st)


def pieces_kernel(heads, q_ref, kv_ref, mask_ref, o_ref, st_ref):
    step = pl.program_id(0)
    lane = lax.broadcasted_iota(jnp.int32, (QLEN, PAD), 1)

    @pl.when(step == 0)
    def _():
        st_ref[...] = jnp.zeros_like(st_ref)

    for h in range(heads):
        found = []
        stats = st_ref[h]
        for i in range(2):
            block = kv_ref[i, :, h * PAD : (h + 1) * PAD]
            scores = lax.dot_general(
                q_ref[h, i * QLEN : (i + 1) * QLEN, :], block, (((1,), (1,)), ((), ())),
                preferred_element_type=jnp.float32,
            )
            usable = mask_ref[i] > 0.5
            masked = jnp.where(usable, scores, -1e30)
            largest = jnp.max(masked, axis=-1, keepdims=True)
            exponent = jnp.where(usable, jnp.exp(masked - largest), 0.0)
            total = jnp.sum(exponent, axis=-1, keepdims=True)
            r = step * 2 + i
            stats = jnp.where(lane == r, largest, jnp.where(lane == r + DH, total, stats))
            found.append(jnp.dot(exponent.astype(jnp.bfloat16), block, preferred_element_type=jnp.float32))
        st_ref[h] = stats
        o_ref[h] = jnp.where(lane < DH, pltpu.roll(found[1], DH, 1), found[0]).astype(jnp.bfloat16)


def attend_pieces(query, key_value, lengths, n):
    requests, positions, width = key_value.shape
    heads = width // PAD
    start = lax.axis_index("mp") * positions
    usable = (start + jnp.arange(positions, dtype=jnp.int32))[None, :] < lengths[:, None]
    mask = usable.astype(jnp.float32)[:, None, :]
    o, st = pl.pallas_call(
        functools.partial(pieces_kernel, heads),
        grid=(requests // 2,),
        out_shape=(
            jax.ShapeDtypeStruct((heads, requests // 2 * QLEN, PAD), jnp.bfloat16),
            jax.ShapeDtypeStruct((heads, QLEN, PAD), jnp.float32),
        ),
        in_specs=[
            pl.BlockSpec((heads, 2 * QLEN, PAD), lambda r: (0, r, 0)),
            pl.BlockSpec((2, positions, width), lambda r: (r, 0, 0)),
            pl.BlockSpec((2, 1, positions), lambda r: (r, 0, 0)),
        ],
        out_specs=[
            pl.BlockSpec((heads, QLEN, PAD), lambda r: (0, r, 0)),
            pl.BlockSpec((heads, QLEN, PAD), lambda r: (0, 0, 0)),
        ],
        name="pieces",
    )(query, key_value, mask)
    o, st = exchange(o, st, n, 2)
    largest, total = st[:, :, :requests], st[:, :, DH : DH + requests]
    scale = jnp.exp(largest - jnp.max(largest, axis=0, keepdims=True))
    share = scale / jnp.sum(scale * total, axis=0, keepdims=True)
    share = share.transpose(0, 2, 1).reshape(n, requests // 2, 2, QLEN, 1)
    o = o.astype(jnp.float32).reshape(n, requests // 2, QLEN, PAD)
    even = jnp.sum(share[:, :, 0] * o[..., DH:], axis=0)
    odd = jnp.sum(share[:, :, 1] * o[..., :DH], axis=0)
    return jnp.stack([even, odd], axis=1).reshape(requests * QLEN, DH).astype(jnp.bfloat16)


def attend(query, key_value, lengths):
    requests, positions, _ = key_value.shape
    query = query.reshape(requests, QLEN, PAD)
    scores = jnp.einsum("rqd,rsd->rqs", query, key_value, preferred_element_type=jnp.float32)
    usable = (jnp.arange(positions, dtype=jnp.int32)[None, :] < lengths[:, None])[:, None, :]
    masked = jnp.where(usable, scores, -1e30)
    largest = jnp.max(masked, axis=-1, keepdims=True)
    exponent = jnp.where(usable, jnp.exp(masked - largest), 0.0)
    weights = (exponent / jnp.sum(exponent, axis=-1, keepdims=True)).astype(jnp.bfloat16)
    context = jnp.einsum("rqs,rsd->rqd", weights, key_value, preferred_element_type=jnp.float32)
    return context[..., DH:].astype(jnp.bfloat16).reshape(requests * QLEN, DH)


def per_device(
    n,
    hidden,
    norm_gain_attn,
    w_query,
    entering_kv,
    cached_kv,
    enc_lengths,
    w_out,
    norm_gain_ffn,
    w_gate,
    w_up,
    w_down,
):
    width = hidden.shape[1]
    portion = gather(normalize(hidden, norm_gain_attn), n, 0).reshape(-1, width)
    query = jnp.dot(portion, w_query, preferred_element_type=jnp.float32).astype(jnp.bfloat16)
    query = jnp.pad(query, ((0, 0), (0, DH)))
    split_row = query.shape[0] // 2
    all_heads = gather(query[:split_row], n, 1)
    context = jnp.concatenate(
        [
            attend_pieces(all_heads, entering_kv, enc_lengths[0], n),
            attend(query[split_row:], cached_kv, enc_lengths[1]),
        ],
        axis=0,
    )
    attention = scatter(jnp.dot(context, w_out, preferred_element_type=jnp.float32), n, 3)
    residual = (hidden.astype(jnp.float32) + attention).astype(jnp.bfloat16)
    portion = gather(normalize(residual, norm_gain_ffn), n, 4).reshape(-1, width)
    gate = jnp.dot(portion, w_gate, preferred_element_type=jnp.float32)
    upward = jnp.dot(portion, w_up, preferred_element_type=jnp.float32)
    activated = (jax.nn.gelu(gate, approximate=True) * upward).astype(jnp.bfloat16)
    feed_out = scatter(jnp.dot(activated, w_down, preferred_element_type=jnp.float32), n, 5)
    return (residual.astype(jnp.float32) + feed_out).astype(jnp.bfloat16)


def solution(mesh):
    placed = (
        P(("groups", "mp"), None),
        P(),
        P(None, "mp"),
        P("groups", "mp", None),
        P("groups", None, "mp"),
        P(None, "groups"),
        P("mp", None),
        P(),
        P(None, "mp"),
        P(None, "mp"),
        P("mp", None),
    )
    return jax.shard_map(
        functools.partial(per_device, mesh.shape["mp"]),
        mesh=mesh,
        in_specs=placed,
        out_specs=P(("groups", "mp"), None),
        check_vma=False,
    )
```

time: 458 us -> 275 us (0.60)
  waiting for transfers between devices: 360 us -> 0 us
  Pallas kernels: 0 us -> 220 us
  local copies, waits for them, and re-layouts: 27.8 us -> 1.82 us
  between operations: 13.2 us -> 0.18 us
  starting transfers between devices: 7.77 us -> 0 us
  other arithmetic: 6.92 us -> 12.9 us
    reduce_scatter x2 -> x0, waiting for transfers between devices: 220 us -> none  [the longest x1 118 us: per_device(): lax.psum_scatter(jnp.dot(context, w_out, preferred_element_type=jnp.float...]
    pallas_call x0 -> x7, Pallas kernels: none -> 220 us  [the longest x2 83 us: scatter(): pl.pallas_call(functools.partial(scatter_kernel, n), out_shape=jax.ShapeD...]
    all_gather x2 -> x0, waiting for transfers between devices: 134 us -> none  [the longest x1 83.9 us: per_device(): lax.all_gather(normalize(hidden, norm_gain_attn), 'mp', axis=0, tiled=True)]
    unnamed x14 -> x8, local copies, waits for them, and re-layouts: 13.3 us -> 0.02 us
    all_to_all x1 -> x0, starting transfers between devices: 7.46 us -> none  [per_device(): lax.all_to_all(entering_kv, 'mp', split_axis=2, concat_axis=1, tiled=True)]
    reshape x1 -> x0, local copies, waits for them, and re-layouts: 7.34 us -> none  [attend(): paired = key_value.reshape(requests, S, head_count, 2, DH)]
    all_to_all x1 -> x0, local copies, waits for them, and re-layouts: 6.84 us -> none  [per_device(): lax.all_to_all(entering_kv, 'mp', split_axis=2, concat_axis=1, tiled=True)]
    all_to_all x1 -> x0, waiting for transfers between devices: 5.75 us -> none  [per_device(): lax.all_to_all(entering_kv, 'mp', split_axis=2, concat_axis=1, tiled=True)]
  transfers between devices with their start and end apart: 5 -> 0, of which waited for: 5 -> 0; matrix products, arithmetic and copies ran while one was open for 4% -> 0% of each run, Pallas kernels for 0% -> 0%
where the time goes in v1:
time: 275 us; the launch traced here: 274 us
  Pallas kernels  220 us (80%)
  matrix products  39 us (14%)
  other arithmetic  12.9 us (5%)
    pallas_call x2, Pallas kernels, scatter(): pl.pallas_call(functools.partial(scatter_kernel, n), out_shape=jax.ShapeD...  83 us
    pallas_call x3, Pallas kernels, gather(): pl.pallas_call(functools.partial(gather_kernel, n), out_shape=jax.ShapeDt...  81.9 us
    pallas_call x1, Pallas kernels, attend_pieces(): pl.pallas_call(functools.partial(pieces_kernel, heads), grid=(requests //...  32.9 us
    pallas_call x1, Pallas kernels, exchange(): pl.pallas_call(functools.partial(exchange_kernel, n), out_shape=(jax.Shap...  22.4 us
    dot_general x1, matrix products, per_device(): jnp.dot(activated, w_down, preferred_element_type=jnp.float32)  17.3 us
    dot_general x1, matrix products, per_device(): gate = jnp.dot(portion, w_gate, preferred_element_type=jnp.float32)  6.76 us

profile of v1, /device:TPU:0, one launch (start us, length us, event | category | flops | bytes accessed | tf_op | source)
XLA Modules:
  0.0 274.2 jit_solution(8228515477980826528)
XLA Ops:
  0.0 0.0 copy-start
  0.0 0.0 copy-start.2
  0.0 1.2 fusion.17
  1.2 0.8 slice_bitcast_fusion.3
  2.0 0.7 compare_convert_fusion.mask_ref
  2.7 0.1 iota_compare_fusion
  2.7 1.8 fusion.19.x_ref
  4.5 35.0 %gather_0.1 = bf16[16,32,4096]{2,1,0:T(8,128)(2,1)} custom-call(bf16[32,4096]{1,0:T(8,128)(2,1)} %fusion.19.x_ref), custom_call_target="tpu_custom_call" | custom-call | tf_op jit(solution)/shard_map/gather_0/pallas_call | solution.py:134
  39.5 0.0 copy-done.2
  39.5 3.6 %convolution_convert_fusion = bf16[512,64]{0,1:T(8,128)(2,1)S(1)} fusion(bf16[512,4096]{1,0:T(8,128)(2,1)} %bitcast.43, bf16[4096,64]{0,1:T(8,128)(2,1)S(1)} %copy-done.2), kind=kOutput, calls=%fused_computation.16 | convolution fusion | flops 268468224 | bytes 4784128 | tf_op jit(solution)/shard_map/dot_general | solution.py:346
  43.1 0.1 copy.19
  43.3 0.7 pad_slice_fusion.1
  43.9 16.0 %gather_1.1.q_ref = bf16[16,256,128]{2,1,0:T(8,128)(2,1)} custom-call(bf16[256,128]{1,0:T(8,128)(2,1)} %get-tuple-element.17.x_ref), custom_call_target="tpu_custom_call" | custom-call | tf_op jit(solution)/shard_map/gather_1/pallas_call | solution.py:134
  59.9 32.9 %pieces.1 = (bf16[16,128,128]{2,1,0:T(8,128)(2,1)}, f32[16,32,128]{2,1,0:T(8,128)}) custom-call(bf16[16,256,128]{2,1,0:T(8,128)(2,1)} %gather_1.1.q_ref, bf16[8,128,2048]{2,1,0:T(8,128)(2,1)} %kv_ref.1, f32[8,1,128]{2,1,0:T(1,128)} %compare_convert_fusion.mask_ref), custom_call_target="tpu_custom_call" | custom-call | tf_op jit(solution)/shard_map/pieces/pallas_call | solution.py:288
  92.9 22.4 %exchange_2.1 = (bf16[16,128,128]{2,1,0:T(8,128)(2,1)}, f32[16,32,128]{2,1,0:T(8,128)}) custom-call(bf16[16,128,128]{2,1,0:T(8,128)(2,1)} %get-tuple-element.9.o_ref, f32[16,32,128]{2,1,0:T(8,128)} %get-tuple-element.10.st_ref), custom_call_target="tpu_custom_call" | custom-call | tf_op jit(solution)/shard_map/exchange_2/pallas_call | solution.py:242
  115.2 1.0 slice_reduce_fusion
  116.2 1.2 multiply_reduce_fusion
  117.4 1.0 divide_bitcast_fusion
  118.4 0.1 copy.21
  118.6 1.2 bitcast_convert_fusion
  119.7 1.0 fusion.14
  120.8 3.9 %fusion.35 = (f32[8,32]{1,0:T(8,128)S(1)}, f32[8,32,2048]{2,1,0:T(8,128)S(1)}) fusion(pred[8,2048]{1,0:T(8,128)(4,1)S(1)} %iota_compare_fusion, bf16[8,32,128]{2,1,0:T(8,128)(2,1)S(1)} %bitcast.46, bf16[8,2048,128]{2,1,0:T(8,128)(2,1)} %param.15), kind=kOutput, calls=%fused_computation.67 | convolution fusion | flops 136316928 | bytes 6374400 | tf_op jit(solution)/shard_map/sub | solution.py:324
  124.7 3.0 %fusion.12 = bf16[8,32,128]{2,1,0:T(8,128)(2,1)S(1)} fusion(bf16[8,2048,128]{2,1,0:T(8,128)(2,1)} %param.15, f32[8,32,2048]{2,1,0:T(8,128)S(1)} %get-tuple-element.24, f32[8,32]{1,0:T(8,128)S(1)} %get-tuple-element.23), kind=kOutput, calls=%fused_computation.17 | convolution fusion | flops 135266304 | bytes 6358016 | tf_op jit(solution)/shard_map/rqs,rsd->rqd/dot_general | solution.py:326
  127.7 0.1 slice.70
  127.8 0.0 copy-done
  127.8 4.5 %fusion.25 = f32[512,4096]{1,0:T(8,128)} fusion(bf16[64,4096]{1,0:T(8,128)(2,1)S(1)} %copy-done, bf16[256,64]{1,0:T(8,128)(2,1)S(1)} %bitcast.45, bf16[256,64]{1,0:T(8,128)(2,1)S(1)} %bitcast.44), kind=kOutput, calls=%fused_computation.43 | convolution fusion | flops 268566528 | bytes 8978432 | tf_op jit(solution)/shard_map/dot_general | solution.py:357
  132.2 0.0 copy-start.1
  132.2 0.0 copy-start.3
  132.2 42.7 %scatter_3.1 = f32[32,4096]{1,0:T(8,128)} custom-call(f32[16,32,4096]{2,1,0:T(8,128)} %bitcast.40), custom_call_target="tpu_custom_call" | custom-call | tf_op jit(solution)/shard_map/scatter_3/pallas_call | solution.py:200
  175.0 0.0 copy-done.1
  175.0 1.2 fusion.21
  176.2 0.0 copy-done.3
  176.2 0.8 fusion.23.x_ref
  177.0 31.0 %gather_4.1 = bf16[16,32,4096]{2,1,0:T(8,128)(2,1)} custom-call(bf16[32,4096]{1,0:T(8,128)(2,1)} %fusion.23.x_ref), custom_call_target="tpu_custom_call" | custom-call | tf_op jit(solution)/shard_map/gather_4/pallas_call | solution.py:134
  208.0 6.8 %fusion.36 = f32[512,640]{1,0:T(8,128)S(1)} fusion(bf16[512,4096]{1,0:T(8,128)(2,1)} %bitcast.41, bf16[4096,640]{1,0:T(8,128)(2,1)} %param.19), kind=kOutput, calls=%fused_computation.68 | convolution fusion | flops 2684354560 | bytes 10747904 | tf_op jit(solution)/shard_map/dot_general | solution.py:360
  214.8 17.3 %fusion.16 = f32[512,4096]{1,0:T(8,128)} fusion(bf16[640,4096]{1,0:T(8,128)(2,1)} %param.21, bf16[512,4096]{1,0:T(8,128)(2,1)} %bitcast.42, bf16[4096,640]{1,0:T(8,128)(2,1)} %param.20, f32[512,640]{1,0:T(8,128)S(1)} %fusion.36), kind=kOutput, calls=%fused_computation.29 | convolution fusion | flops 5371985920 | bytes 24379392 | tf_op jit(solution)/shard_map/dot_general | solution.py:363
  232.1 40.3 %scatter_5.1 = f32[32,4096]{1,0:T(8,128)} custom-call(f32[16,32,4096]{2,1,0:T(8,128)} %bitcast.39), custom_call_target="tpu_custom_call" | custom-call | tf_op jit(solution)/shard_map/scatter_5/pallas_call | solution.py:200
  272.4 1.8 fusion.24
  (8 shorter events, 0.1 us)
Async XLA Ops:
  0.0 127.8 %copy-start = (bf16[64,4096]{1,0:T(8,128)(2,1)S(1)}, bf16[64,4096]{1,0:T(8,128)(2,1)}, u32[]{:S(2)}) copy-start(bf16[64,4096]{1,0:T(8,128)(2,1)} %param.17) | copy-start | bytes 1572868
  0.0 39.5 %copy-start.2 = (bf16[4096,64]{0,1:T(8,128)(2,1)S(1)}, bf16[4096,64]{0,1:T(8,128)(2,1)}, u32[]{:S(2)}) copy-start(bf16[4096,64]{0,1:T(8,128)(2,1)} %param.13) | copy-start | bytes 1572868
  132.2 42.7 %copy-start.1 = (bf16[32,4096]{1,0:T(8,128)(2,1)S(1)}, bf16[32,4096]{1,0:T(8,128)(2,1)}, u32[]{:S(2)}) copy-start(bf16[32,4096]{1,0:T(8,128)(2,1)} %param.11) | copy-start | bytes 786436
  132.2 44.0 %copy-start.3 = (f32[4096]{0:T(1024)S(1)}, f32[4096]{0:T(1024)}, u32[]{:S(2)}) copy-start(f32[4096]{0:T(1024)} %param.18) | copy-start | bytes 49156

commit v2 on v1

v2 whole, which is shorter than its diff:
```python
import functools

import jax
import jax.numpy as jnp
from jax import lax
from jax.experimental import pallas as pl
from jax.experimental.pallas import tpu as pltpu
from jax.sharding import PartitionSpec as P

DH = 64
QLEN = 32
PAD = 2 * DH
MESH = pl.DeviceIdType.MESH
VM = pltpu.VMEM
DMA = pltpu.SemaphoreType.DMA

epsilon = 0.1


def normalize(matrix, gain_row):
    values = matrix.astype(jnp.float32)
    mean_square = jnp.mean(values * values, axis=-1, keepdims=True)
    return (values * lax.rsqrt(mean_square + epsilon) * gain_row).astype(jnp.bfloat16)


def place(n):
    me = lax.axis_index("mp")
    return me, me // 4, (me // 2) % 2, me % 2


def index_of(a, b, c):
    return (a * 2 + b) * 2 + c


def remote(src, dst, send, recv, to):
    return pltpu.make_async_remote_copy(
        src_ref=src, dst_ref=dst, send_sem=send, recv_sem=recv, device_id={"mp": to}, device_id_type=MESH
    )


def greet(to):
    pl.semaphore_signal(pltpu.get_barrier_semaphore(), inc=1, device_id={"mp": to}, device_id_type=MESH)


def gather_kernel(n, x_ref, out_ref, zs, zr, ys, yr, cs, cr):
    A = n // 4
    me, a, b, c = place(n)
    across, pair = index_of(a, 1 - b, c), index_of(a, b, 1 - c)
    right, left = me + 4, me - 4
    has = {1: a < A - 1, -1: a > 0}
    toward = {1: right, -1: left}
    for d in (1, -1):

        @pl.when(has[d])
        def _():
            greet(toward[d])

    greet(across)
    greet(pair)
    pl.semaphore_wait(
        pltpu.get_barrier_semaphore(), 2 + has[1].astype(jnp.int32) + has[-1].astype(jnp.int32)
    )

    def z_copy(src, k, s, d):
        row = 0 if d == 1 else A
        return remote(src, out_ref.at[index_of(k, b, c)], zs.at[row + s], zr.at[k], toward[d])

    def y_copy(src, k, bb):
        return remote(src, out_ref.at[index_of(k, bb, c)], ys.at[k], yr.at[k], across)

    def c_copy(src, k, bb, cc):
        return remote(src, out_ref.at[index_of(k, bb, cc)], cs.at[bb * A + k], cr.at[bb * A + k], pair)

    for d in (1, -1):

        @pl.when(has[d])
        def _():
            z_copy(x_ref, a, 0, d).start()

    y_copy(x_ref, a, b).start()
    c_copy(x_ref, a, b, c).start()
    out_ref[me] = x_ref[...]

    def pass_on(s):
        for d in (1, -1) if s else (1,):
            k = a - s * d

            @pl.when((k >= 0) & (k < A))
            def _():
                y_copy(x_ref, k, 1 - b).wait_recv()
                c_copy(out_ref.at[index_of(k, 1 - b, c)], k, 1 - b, c).start()

    for s in range(1, A):
        for d in (1, -1):
            k = a - s * d

            @pl.when((k >= 0) & (k < A))
            def _():
                block = out_ref.at[index_of(k, b, c)]
                remote(x_ref, block, zs.at[0], zr.at[k], toward[-d]).wait_recv()

                @pl.when(has[d])
                def _():
                    z_copy(block, k, s, d).start()

                y_copy(block, k, b).start()
                c_copy(block, k, b, c).start()

        pass_on(s - 1)
    pass_on(A - 1)
    for bb in range(2):
        for k in range(A):
            c_copy(x_ref, k, bb, 1 - c).wait_recv()
    for s in range(A):
        for d in (1, -1):
            k = a - s * d

            @pl.when((k >= 0) & (k < A) & has[d])
            def _():
                z_copy(x_ref, k, s, d).wait_send()

    for k in range(A):
        y_copy(x_ref, k, b).wait_send()
        for bb in range(2):
            c_copy(x_ref, k, bb, c).wait_send()


def params(number):
    return pltpu.CompilerParams(collective_id=number, has_side_effects=True, vmem_limit_bytes=56 * 2**20)


def gather(x, n, number):
    A = n // 4
    return pl.pallas_call(
        functools.partial(gather_kernel, n),
        out_shape=jax.ShapeDtypeStruct((n,) + x.shape, x.dtype),
        in_specs=[pl.BlockSpec(memory_space=VM)],
        out_specs=pl.BlockSpec(memory_space=VM),
        scratch_shapes=[DMA((2 * A,)), DMA((A,)), DMA((A,)), DMA((A,)), DMA((2 * A,)), DMA((2 * A,))],
        compiler_params=params(number),
        name=f"gather_{number}",
    )(x)


def scatter_kernel(
    n, left_ref, w_ref, out_ref, part, cbuf, ysend, yrecv, zsend, zright, zleft, cs, cr, ys, yr, zs, zr
):
    A = n // 4
    me, a, b, c = place(n)
    across, pair = index_of(a, 1 - b, c), index_of(a, b, 1 - c)
    has = {1: a < A - 1, -1: a > 0}
    toward = {1: me + 4, -1: me - 4}
    landing = {1: zright, -1: zleft}
    rows, width = out_ref.shape
    for d in (1, -1):

        @pl.when(has[d])
        def _():
            greet(toward[d])

    greet(across)
    greet(pair)
    pl.semaphore_wait(
        pltpu.get_barrier_semaphore(), 2 + has[1].astype(jnp.int32) + has[-1].astype(jnp.int32)
    )

    def near_last(visit):
        for s in range(A - 1, -1, -1):
            for d in (1, -1) if s else (1,):
                k = a + s * d

                @pl.when((k >= 0) & (k < A))
                def _():
                    visit(s, d, k)

    def multiply(group, bb, cc):
        left = jnp.concatenate([left_ref[index_of(k, bb, cc)] for k in range(A)], axis=0)
        tile = min(width, 1024)

        def columns(t, carry):
            at = pl.ds(pl.multiple_of(t * tile, tile), tile)
            found = jnp.dot(left, w_ref[:, at], preferred_element_type=jnp.float32)
            part[group, :, :, at] = found.reshape(A, rows, tile)
            return carry

        lax.fori_loop(0, width // tile, columns, 0)

    def c_copy(group, k, bb):
        slot = bb * A + k
        return remote(part.at[group, k], cbuf.at[slot], cs.at[slot], cr.at[slot], pair)

    def y_copy(k):
        return remote(ysend.at[k], yrecv.at[k], ys.at[k], yr.at[k], across)

    def z_copy(k, d):
        row = 0 if d == 1 else A
        return remote(zsend.at[k], landing[d].at[k], zs.at[k], zr.at[row + k], toward[d])

    def z_arrival(k, d):
        row = 0 if d == 1 else A
        return remote(zsend.at[k], landing[d].at[k], zs.at[k], zr.at[row + k], toward[-d])

    multiply(0, 1 - b, 1 - c)
    near_last(lambda s, d, k: c_copy(0, k, 1 - b).start())
    multiply(1, 1 - b, c)

    def send_across(s, d, k):
        c_copy(0, k, 1 - b).wait_recv()
        ysend[k] = (part[1, k] + cbuf[(1 - b) * A + k]).astype(jnp.bfloat16)
        y_copy(k).start()

    near_last(send_across)
    multiply(2, b, 1 - c)
    near_last(lambda s, d, k: c_copy(2, k, b).start())
    multiply(3, b, c)

    def pass_on(s, d, k):
        c_copy(2, k, b).wait_recv()
        y_copy(k).wait_recv()
        part[3, k] = part[3, k] + cbuf[b * A + k] + yrecv[k].astype(jnp.float32)
        for came in (d,) if s else (1, -1):

            @pl.when(has[-came])
            def _():
                z_arrival(k, came).wait_recv()
                part[3, k] = part[3, k] + landing[came][k].astype(jnp.float32)

        if s:
            zsend[k] = part[3, k].astype(jnp.bfloat16)
            z_copy(k, d).start()
        else:
            out_ref[...] = part[3, k]

    near_last(pass_on)

    def finish(s, d, k):
        y_copy(k).wait_send()
        if s:
            z_copy(k, d).wait_send()
        c_copy(0, k, 1 - b).wait_send()
        c_copy(2, k, b).wait_send()

    near_last(finish)


def scatter(left, w, n, number):
    A = n // 4
    rows, depth = left.shape[0] // n, left.shape[1]
    block = (rows, w.shape[1])
    half = jnp.bfloat16
    return pl.pallas_call(
        functools.partial(scatter_kernel, n),
        out_shape=jax.ShapeDtypeStruct(block, jnp.float32),
        in_specs=[pl.BlockSpec(memory_space=VM)] * 2,
        out_specs=pl.BlockSpec(memory_space=VM),
        scratch_shapes=[VM((4, A) + block, jnp.float32), VM((2 * A,) + block, jnp.float32)]
        + [VM((A,) + block, half)] * 5
        + [DMA((2 * A,)), DMA((2 * A,)), DMA((A,)), DMA((A,)), DMA((A,)), DMA((2 * A,))],
        compiler_params=params(number),
        name=f"scatter_{number}",
    )(left.reshape(n, rows, depth), w)


def attend_kernel(
    n, q_ref, own_ref, kv_ref, cached_ref, mask_ref, cached_mask_ref, out_ref,
    q_all, kv, cached, scores, chances, o_send, o_recv, st_send, st_recv, local, qs, qr, os, orr, ss, sr,
):
    me = lax.axis_index("mp")
    requests, positions, width = kv.shape
    pairs, heads = requests // 2, width // PAD
    load_cached = pltpu.make_async_copy(cached_ref, cached, local.at[0])
    load_kv = pltpu.make_async_copy(kv_ref, kv, local.at[1])
    load_cached.start()
    load_kv.start()
    order = sorted(range(1, n), key=lambda s: -min(s, n - s))
    others = [lax.rem(me + s, n) for s in order]
    for other in others:
        greet(other)
    pl.semaphore_wait(pltpu.get_barrier_semaphore(), n - 1)

    def q_copy(other, spot):
        return remote(q_ref, q_all.at[spot], qs.at[other], qr.at[spot], other)

    def o_copy(other, spot, step):
        rows = pl.ds(pl.multiple_of(step * QLEN, QLEN), QLEN)
        return remote(
            o_send.at[other, rows], o_recv.at[spot, rows], os.at[step, other], orr.at[step, spot], other
        )

    def st_copy(other, spot):
        return remote(st_send.at[other], st_recv.at[spot], ss.at[other], sr.at[spot], other)

    for other in others:
        q_copy(other, me).start()
    q_all[me] = q_ref[...]
    lane = lax.broadcasted_iota(jnp.int32, (QLEN, PAD), 1)
    load_cached.wait()

    def cached_request(r, carry):
        rows = pl.ds(pl.multiple_of(r * QLEN, QLEN), QLEN)
        block = cached[r]
        found = lax.dot_general(
            own_ref[rows, :], block, (((1,), (1,)), ((), ())), preferred_element_type=jnp.float32
        )
        usable = cached_mask_ref[r] > 0.5
        masked = jnp.where(usable, found, -1e30)
        exponent = jnp.where(usable, jnp.exp(masked - jnp.max(masked, axis=-1, keepdims=True)), 0.0)
        weights = (exponent / jnp.sum(exponent, axis=-1, keepdims=True)).astype(jnp.bfloat16)
        to = pl.ds(pl.multiple_of((requests + r) * QLEN, QLEN), QLEN)
        out_ref[to, :] = jnp.dot(weights, block, preferred_element_type=jnp.float32).astype(jnp.bfloat16)
        return carry

    lax.fori_loop(0, requests, cached_request, 0)
    st_send[...] = jnp.zeros_like(st_send)
    load_kv.wait()
    for other in others:
        q_copy(other, other).wait_recv()

    def pair_step(step, carry):
        rows = pl.ds(pl.multiple_of(step * QLEN, QLEN), QLEN)
        low = lane < DH
        nothing = jnp.zeros((QLEN, PAD), jnp.bfloat16)
        for i in range(2):
            for g in range(heads // 2):
                two = []
                for h in (2 * g, 2 * g + 1):
                    packed = q_all[h, rows, :].astype(jnp.float32)
                    packed = packed if i == 0 else pltpu.roll(packed, DH, 1)
                    two.append(jnp.where(low, packed, 0.0).astype(jnp.bfloat16))
                spread = jnp.concatenate(
                    [
                        jnp.concatenate([two[0], nothing], axis=1),
                        jnp.concatenate([nothing, two[1]], axis=1),
                    ],
                    axis=0,
                )
                scores[i, g] = lax.dot_general(
                    spread, kv[step * 2 + i, :, g * 2 * PAD : (g + 1) * 2 * PAD], (((1,), (1,)), ((), ())),
                    preferred_element_type=jnp.float32,
                )
        for i in range(2):
            r = step * 2 + i
            usable = mask_ref[r] > 0.5
            masked = jnp.where(usable, scores[i], -1e30)
            largest = jnp.max(masked, axis=-1, keepdims=True)
            exponent = jnp.where(usable, jnp.exp(masked - largest), 0.0)
            total = jnp.sum(exponent, axis=-1, keepdims=True)
            chances[i] = exponent.astype(jnp.bfloat16)
            st_send[...] = jnp.where(
                lane == r,
                largest.reshape(heads, QLEN, 1),
                jnp.where(lane == r + DH, total.reshape(heads, QLEN, 1), st_send[...]),
            )
        for g in range(heads // 2):
            found = [
                jnp.dot(
                    chances[i, g], kv[step * 2 + i, :, g * 2 * PAD : (g + 1) * 2 * PAD],
                    preferred_element_type=jnp.float32,
                )
                for i in range(2)
            ]
            for e in range(2):
                even, odd = (f[e * QLEN : (e + 1) * QLEN, e * PAD : (e + 1) * PAD] for f in found)
                o_send[2 * g + e, rows, :] = jnp.where(low, pltpu.roll(odd, DH, 1), even).astype(jnp.bfloat16)
        for other in others:
            o_copy(other, me, step).start()
        return carry

    lax.fori_loop(0, pairs, pair_step, 0)
    for other in others:
        st_copy(other, me).start()
    o_recv[me] = o_send[me]
    st_recv[me] = st_send[me]
    for other in others:
        st_copy(other, other).wait_recv()
    largest = st_recv[...]
    scale = jnp.exp(largest - jnp.max(largest, axis=0, keepdims=True))
    total = jnp.sum(
        scale * pltpu.roll(largest.reshape(n * QLEN, PAD), DH, 1).reshape(n, QLEN, PAD), axis=0, keepdims=True
    )
    st_recv[...] = scale / jnp.where(total > 0.0, total, 1.0)
    for step in range(pairs):
        for other in others:
            o_copy(other, other, step).wait_recv()
        mixed = jnp.zeros((QLEN, PAD), jnp.float32)
        for d in range(n):
            share = st_recv[d]
            share = jnp.where(
                lane < DH, share[:, 2 * step + 1 : 2 * step + 2], share[:, 2 * step : 2 * step + 1]
            )
            mixed = mixed + share * o_recv[d, step * QLEN : (step + 1) * QLEN, :].astype(jnp.float32)
        out_ref[2 * step * QLEN : (2 * step + 1) * QLEN, :] = mixed.astype(jnp.bfloat16)
        out_ref[(2 * step + 1) * QLEN : (2 * step + 2) * QLEN, :] = pltpu.roll(mixed, DH, 1).astype(jnp.bfloat16)
    for other in others:
        q_copy(other, me).wait_send()
        st_copy(other, me).wait_send()
        for step in range(pairs):
            o_copy(other, me, step).wait_send()


def attend(query, entering_kv, cached_kv, lengths, n, number):
    requests, positions, width = entering_kv.shape
    length = cached_kv.shape[1]
    pairs, heads = requests // 2, width // PAD
    half = query.shape[0] // 2
    packed = query[:half].reshape(pairs, 2, QLEN, DH)
    packed = jnp.concatenate([packed[:, 0], packed[:, 1]], axis=-1).reshape(pairs * QLEN, PAD)
    own = jnp.pad(query[half:], ((0, 0), (0, DH)))
    start = lax.axis_index("mp") * positions
    usable = (start + jnp.arange(positions, dtype=jnp.int32))[None, :] < lengths[0][:, None]
    cached_usable = jnp.arange(length, dtype=jnp.int32)[None, :] < lengths[1][:, None]
    half_type = jnp.bfloat16
    context = pl.pallas_call(
        functools.partial(attend_kernel, n),
        out_shape=jax.ShapeDtypeStruct((2 * requests * QLEN, PAD), half_type),
        in_specs=[pl.BlockSpec(memory_space=m) for m in (VM, VM, pl.ANY, pl.ANY, VM, VM)],
        out_specs=pl.BlockSpec(memory_space=VM),
        scratch_shapes=[
            VM((n,) + packed.shape, half_type),
            VM(entering_kv.shape, half_type),
            VM(cached_kv.shape, half_type),
            VM((2, heads // 2, 2 * QLEN, positions), jnp.float32),
            VM((2, heads // 2, 2 * QLEN, positions), half_type),
            VM((n, pairs * QLEN, PAD), half_type),
            VM((n, pairs * QLEN, PAD), half_type),
            VM((n, QLEN, PAD), jnp.float32),
            VM((n, QLEN, PAD), jnp.float32),
            DMA((2,)), DMA((n,)), DMA((n,)), DMA((pairs, n)), DMA((pairs, n)), DMA((n,)), DMA((n,)),
        ],
        compiler_params=params(number),
        name=f"attend_{number}",
    )(
        packed, own, entering_kv, cached_kv,
        usable.astype(jnp.float32)[:, None, :], cached_usable.astype(jnp.float32)[:, None, :],
    )
    return context[:, DH:]


def per_device(
    n,
    hidden,
    norm_gain_attn,
    w_query,
    entering_kv,
    cached_kv,
    enc_lengths,
    w_out,
    norm_gain_ffn,
    w_gate,
    w_up,
    w_down,
):
    width = hidden.shape[1]
    portion = gather(normalize(hidden, norm_gain_attn), n, 0).reshape(-1, width)
    query = jnp.dot(portion, w_query, preferred_element_type=jnp.float32).astype(jnp.bfloat16)
    context = attend(query, entering_kv, cached_kv, enc_lengths, n, 1)
    attention = scatter(context, w_out, n, 3)
    residual = (hidden.astype(jnp.float32) + attention).astype(jnp.bfloat16)
    portion = gather(normalize(residual, norm_gain_ffn), n, 4).reshape(-1, width)
    gate = jnp.dot(portion, w_gate, preferred_element_type=jnp.float32)
    upward = jnp.dot(portion, w_up, preferred_element_type=jnp.float32)
    activated = (jax.nn.gelu(gate, approximate=True) * upward).astype(jnp.bfloat16)
    feed_out = scatter(activated, w_down, n, 5)
    return (residual.astype(jnp.float32) + feed_out).astype(jnp.bfloat16)


def solution(mesh):
    placed = (
        P(("groups", "mp"), None),
        P(),
        P(None, "mp"),
        P("groups", "mp", None),
        P("groups", None, "mp"),
        P(None, "groups"),
        P("mp", None),
        P(),
        P(None, "mp"),
        P(None, "mp"),
        P("mp", None),
    )
    return jax.shard_map(
        functools.partial(per_device, mesh.shape["mp"]),
        mesh=mesh,
        in_specs=placed,
        out_specs=P(("groups", "mp"), None),
        check_vma=False,
    )
```

time: 275 us -> 205 us (0.75)
  Pallas kernels: 220 us -> 177 us
  matrix products: 39 us -> 15.8 us
  other arithmetic: 12.9 us -> 8.91 us
    dot_general x3 -> x1, matrix products: 24.7 us -> 6.89 us  [per_device(): upward = jnp.dot(portion, w_up, preferred_element_type=jnp.float32)]
    pallas_call x2 -> x1, Pallas kernels: 55.3 us -> 38.3 us  [attend(): pl.pallas_call(functools.partial(attend_kernel, n), out_shape=jax.ShapeDt...]
    pallas_call x3 -> x2, Pallas kernels: 81.9 us -> 66.9 us  [gather(): pl.pallas_call(functools.partial(gather_kernel, n), out_shape=jax.ShapeDt...]
    pallas_call x2, Pallas kernels: 83 us -> 71.7 us  [scatter(): pl.pallas_call(functools.partial(scatter_kernel, n), out_shape=jax.ShapeD...]
    sub x1 -> x0, matrix products: 3.93 us -> none  [attend(): exponent = jnp.where(usable, jnp.exp(masked - largest), 0.0)]
where the time goes in v2:
time: 205 us
  Pallas kernels  177 us (86%)
  matrix products  15.8 us (8%)
  other arithmetic  8.91 us (4%)
  local copies, waits for them, and re-layouts  3.12 us (2%)
    pallas_call x2, Pallas kernels, scatter(): pl.pallas_call(functools.partial(scatter_kernel, n), out_shape=jax.ShapeD...  71.7 us
    pallas_call x2, Pallas kernels, gather(): pl.pallas_call(functools.partial(gather_kernel, n), out_shape=jax.ShapeDt...  66.9 us
    pallas_call x1, Pallas kernels, attend(): pl.pallas_call(functools.partial(attend_kernel, n), out_shape=jax.ShapeDt...  38.3 us
    dot_general x1, matrix products, per_device(): upward = jnp.dot(portion, w_up, preferred_element_type=jnp.float32)  6.89 us
    dot_general x1, matrix products, per_device(): gate = jnp.dot(portion, w_gate, preferred_element_type=jnp.float32)  5.46 us

profile of v2, /device:TPU:0, one launch (start us, length us, event | category | flops | bytes accessed | tf_op | source)
XLA Modules:
  0.0 204.9 jit_solution(7742363975634259463)
XLA Ops:
  0.0 0.0 copy-start
  0.0 1.2 fusion.8
  1.2 0.8 slice_bitcast_fusion
  2.0 0.7 compare_convert_fusion.1.mask_ref
  2.6 0.7 compare_convert_fusion.cached_mask_ref
  3.3 1.8 fusion.10.x_ref
  5.1 35.0 %gather_0.1 = bf16[16,32,4096]{2,1,0:T(8,128)(2,1)} custom-call(bf16[32,4096]{1,0:T(8,128)(2,1)} %fusion.10.x_ref), custom_call_target="tpu_custom_call" | custom-call | tf_op jit(solution)/shard_map/gather_0/pallas_call | solution.py:134
  40.2 0.0 copy-done
  40.2 3.4 %convolution_convert_fusion = bf16[512,64]{1,0:T(8,128)(2,1)S(1)} fusion(bf16[512,4096]{1,0:T(8,128)(2,1)} %bitcast.20, bf16[4096,64]{0,1:T(8,128)(2,1)S(1)} %copy-done), kind=kOutput, calls=%fused_computation.10 | convolution fusion | flops 268468224 | bytes 4784128 | tf_op jit(solution)/shard_map/dot_general | solution.py:455
  43.6 0.6 pad.4.own_ref
  44.3 0.0 slice-start
  44.3 0.7 pad_maximum_fusion.q_ref
  45.0 0.0 copy-start.2
  45.0 0.0 copy-start.3
  45.0 0.0 slice-start.1
  45.0 38.3 %attend_1.1 = bf16[512,128]{1,0:T(8,128)(2,1)} custom-call(bf16[128,128]{1,0:T(8,128)(2,1)} %pad_maximum_fusion.q_ref, bf16[256,128]{1,0:T(8,128)(2,1)} %pad.4.own_ref, bf16[8,128,2048]{2,1,0:T(8,128)(2,1)} %kv_ref.1, bf16[8,2048,128]{2,1,0:T(8,128)(2,1)} %cached_ref.1, f32[8,1,128]{2,1,0:T(1,128)} %compare_convert_fusion.1.mask_ref, ...), custom_call_target="tpu_custom_call" | custom-call | tf_op jit(solution)/shard_map/attend_1/pallas_call | solution.py:413
  83.3 1.7 slice.27
  84.9 36.3 %scatter_3.1 = f32[32,4096]{1,0:T(8,128)} custom-call(bf16[16,32,64]{2,1,0:T(8,128)(2,1)} %bitcast.22, bf16[64,4096]{1,0:T(8,128)(2,1)} %w_ref.2), custom_call_target="tpu_custom_call" | custom-call | tf_op jit(solution)/shard_map/scatter_3/pallas_call | solution.py:251
  121.3 0.0 copy-done.2
  121.3 1.2 fusion.12
  122.5 0.0 copy-done.3
  122.5 0.8 fusion.14.x_ref
  123.4 31.9 %gather_4.1 = bf16[16,32,4096]{2,1,0:T(8,128)(2,1)} custom-call(bf16[32,4096]{1,0:T(8,128)(2,1)} %fusion.14.x_ref), custom_call_target="tpu_custom_call" | custom-call | tf_op jit(solution)/shard_map/gather_4/pallas_call | solution.py:134
  155.2 0.0 slice-done
  155.2 0.0 slice-done.1
  155.3 0.0 copy-start.1
  155.3 5.5 %fusion.19 = f32[512,640]{1,0:T(8,128)S(1)} fusion(bf16[512,4096]{1,0:T(8,128)(2,1)} %bitcast.18, bf16[4096,640]{1,0:T(8,128)(2,1)S(1)} %bitcast.28), kind=kOutput, calls=%fused_computation.35 | convolution fusion | flops 2684354560 | bytes 10747904 | tf_op jit(solution)/shard_map/dot_general | solution.py:460
  160.7 0.0 copy-done.1
  160.8 6.9 %fusion = bf16[512,640]{1,0:T(8,128)(2,1)} fusion(bf16[512,4096]{1,0:T(8,128)(2,1)S(1)} %bitcast.19, bf16[4096,640]{1,0:T(8,128)(2,1)} %param.20, f32[512,640]{1,0:T(8,128)S(1)} %fusion.19), kind=kOutput, calls=%fused_computation.2 | convolution fusion | flops 2687631360 | bytes 11403264 | tf_op jit(solution)/shard_map/dot_general | solution.py:461
  167.6 35.4 %scatter_5.1 = f32[32,4096]{1,0:T(8,128)} custom-call(bf16[16,32,640]{2,1,0:T(8,128)(2,1)} %bitcast.21, bf16[640,4096]{1,0:T(8,128)(2,1)} %w_ref.3), custom_call_target="tpu_custom_call" | custom-call | tf_op jit(solution)/shard_map/scatter_5/pallas_call | solution.py:251
  203.1 1.8 fusion.15
  (7 shorter events, 0.0 us)
Async XLA Ops:
  0.0 40.2 %copy-start = (bf16[4096,64]{0,1:T(8,128)(2,1)S(1)}, bf16[4096,64]{0,1:T(8,128)(2,1)}, u32[]{:S(2)}) copy-start(bf16[4096,64]{0,1:T(8,128)(2,1)} %param.13) | copy-start | bytes 1572868
  44.3 111.0 %slice-start = ((s8[5242880]{0:T(1024)(128)(4,1)}), s8[4194304]{0:T(1024)(128)(4,1)S(1)}, s32[]{:S(2)}) async-start(s8[5242880]{0:T(1024)(128)(4,1)} %bitcast.27), calls=%async_computation | async-start | bytes 8388608
  45.0 76.3 %copy-start.2 = (bf16[32,4096]{1,0:T(8,128)(2,1)S(1)}, bf16[32,4096]{1,0:T(8,128)(2,1)}, u32[]{:S(2)}) copy-start(bf16[32,4096]{1,0:T(8,128)(2,1)} %param.11) | copy-start | bytes 786436
  45.0 77.6 %copy-start.3 = (f32[4096]{0:T(1024)S(1)}, f32[4096]{0:T(1024)}, u32[]{:S(2)}) copy-start(f32[4096]{0:T(1024)} %param.18) | copy-start | bytes 49156
  45.0 110.3 %slice-start.1 = ((s8[5242880]{0:T(1024)(128)(4,1)}), s8[1048576]{0:T(1024)(128)(4,1)S(1)}, s32[]{:S(2)}) async-start(s8[5242880]{0:T(1024)(128)(4,1)} %bitcast.27), calls=%async_computation.1 | async-start | bytes 2097152
  155.3 5.5 %copy-start.1 = (bf16[16,32,4096]{2,1,0:T(8,128)(2,1)S(1)}, bf16[16,32,4096]{2,1,0:T(8,128)(2,1)}, u32[]{:S(2)}) copy-start(bf16[16,32,4096]{2,1,0:T(8,128)(2,1)} %gather_4.1) | copy-start | bytes 12582916
